TPU v7x, 32 devices: a whole 2x2x4 slice. The times are simulated.
32 devices in a mesh: seq: 16 (over z, y, x), tp: 2 (over core).
Axes of the slice: x: 2, y: 2, z: 4, core: 2. Of those that a mesh axis runs over, the one named last changes fastest.
Arguments:
- img: bfloat16 [4, 512, 3072], P(None, 'seq', 'tp'), may hold values from -6 to 6
- txt: bfloat16 [4, 64, 3072], P(None, 'seq', 'tp'), may hold values from -6 to 6
- prev_mod: bfloat16 [4, 512, 3072], P(None, 'seq', 'tp'), may hold values from -47 to 47
- cache: float32 [4, 512, 3072], P(None, 'seq', 'tp'), may hold values from -6 to 6
- modulation: bfloat16 [3, 4, 3072], P(None, None, 'tp'), may hold values from -4 to 4
- w_qkv: bfloat16 [3072, 3, 2048], P('seq', None, 'tp'), may hold values from -1 to 1, as said below
- qk_gain: float32 [2, 2048], P(None, 'tp'), may hold values from 0.5 to 6, as said below
- output_weight: bfloat16 [2048, 3072], P('tp'), may hold values from -0.1875 to 0.1875
- text_len: int32 [4], replicated, may hold values from 1 to 64
- refresh: int32 [4], replicated, may hold values from 0 to 1, as said below
Outputs:
- out_img: float32 [4, 512, 3072], P(None, 'seq', 'tp')
- new_cache: float32 [4, 512, 3072], P(None, 'seq', 'tp')
- rel_l1: float32 [4], replicated
Inputs may be any that keep to these rules, and one draw needn't show every extreme that they name: `refresh`: at least one sequence has flag 1 and at least one has flag 0. `w_qkv`: entries of spread about one over the square root of 3072. `qk_gain`: positive.
All inputs are finite; a program needn't handle non-finite values.
Results may differ from a plain program's by a relative error of at most 0.013.
The roundings to bfloat16 on the way count: a program that leaves them out, or rounds other values in their place, can miss the bound.
Values may be sent and summed in bfloat16 or wider, within the bound.
A program may use at most 128 MiB of HBM per device.

v0:
```python
import jax
import jax.numpy as jnp
from jax import lax
from jax.sharding import PartitionSpec as P

HD = 128
EPS = 0.1
NEG = -1e30


def unit_heads(block, gain):
    shaped = block.reshape(block.shape[:-1] + (block.shape[-1] // HD, HD))
    scaled = shaped * lax.rsqrt(jnp.mean(jnp.square(shaped), axis=-1, keepdims=True) + EPS)
    return scaled.reshape(block.shape) * gain


def local(img, txt, prev_mod, cache, modulation, w_qkv, qk_gain, output_weight, text_len, refresh):
    batch, img_rows, width_loc = img.shape
    txt_rows = txt.shape[1]
    rows = txt_rows + img_rows
    joined = jnp.concatenate([txt, img], axis=1)
    local_mods = modulation.astype(jnp.float32)
    wide, wide_mod = (
        lax.all_gather(joined, "tp", axis=2, tiled=True),
        lax.all_gather(modulation, "tp", axis=2, tiled=True),
    )
    wide_mods = wide_mod.astype(jnp.float32)
    values = wide.astype(jnp.float32)
    center = jnp.mean(values, axis=2, keepdims=True)
    spread = jnp.mean(jnp.square(values - center), axis=2, keepdims=True)
    normed = (values - center) * lax.rsqrt(spread + EPS)
    modded = (normed * (1.0 + wide_mods[1][:, None, :]) + wide_mods[0][:, None, :]).astype(
        jnp.bfloat16
    )
    offset = lax.axis_index("tp") * width_loc
    own_image = lax.dynamic_slice_in_dim(modded[:, txt_rows:, :], offset, width_loc, 2)
    previous = prev_mod.astype(jnp.float32)
    gap = jnp.sum(jnp.abs(own_image.astype(jnp.float32) - previous), axis=(1, 2))
    base_sum = jnp.sum(jnp.abs(previous), axis=(1, 2))
    numer, denom = lax.psum((gap, base_sum), ("seq", "tp"))
    rel_l1 = numer / jnp.maximum(denom, 1.0)
    columns = w_qkv.shape[2]
    projected = jnp.einsum(
        "btd,dkc->btkc",
        modded,
        lax.all_gather(w_qkv, "seq", axis=0, tiled=True),
        preferred_element_type=jnp.float32,
    )
    heads = columns // HD
    query = unit_heads(projected[:, txt_rows:, 0, :], qk_gain[0]).astype(jnp.bfloat16)
    query_heads = query.reshape(batch, img_rows, heads, HD)
    keyed = unit_heads(projected[:, :, 1, :], qk_gain[1]).astype(jnp.bfloat16)
    valued = projected[:, :, 2, :].astype(jnp.bfloat16)
    paired = jnp.stack([keyed, valued], axis=2)
    score_scale = 1.0 / HD**0.5
    start_top = jnp.full((batch, heads, img_rows), NEG, jnp.float32)
    piece = lax.all_gather(paired, "seq", axis=1, tiled=True)
    top = start_top
    count = piece.shape[1]
    index = jnp.arange(count, dtype=jnp.int32)
    slot = index % rows
    text_pos = index // rows * txt_rows + slot
    valid = (slot >= txt_rows)[None, :] | (text_pos[None, :] < text_len[:, None])
    keys = piece[:, :, 0, :].reshape(batch, count, heads, HD)
    vals = piece[:, :, 1, :].reshape(batch, count, heads, HD)
    logit_scores = (
        jnp.einsum("bqhc,bkhc->bhqk", query_heads, keys, preferred_element_type=jnp.float32)
        * score_scale
    )
    logit_scores = jnp.where(valid[:, None, None, :], logit_scores, NEG)
    new_top = jnp.maximum(top, jnp.max(logit_scores, axis=3))
    attention_weights = jnp.where(
        valid[:, None, None, :], jnp.exp(logit_scores - new_top[..., None]), 0.0
    )
    total = jnp.sum(attention_weights, axis=3)
    summed_output = jnp.einsum(
        "bhqk,bkhc->bhqc",
        attention_weights.astype(jnp.bfloat16),
        vals,
        preferred_element_type=jnp.float32,
    )
    top, total, summed_output = (new_top, total, summed_output)
    attended_values = (summed_output / total[..., None]).astype(jnp.bfloat16)
    attended_values = attended_values.transpose(0, 2, 1, 3).reshape(batch, img_rows, columns)
    partial_output = jnp.einsum(
        "pxr,ro->pxo", attended_values, output_weight, preferred_element_type=jnp.float32
    )
    whole = lax.psum(partial_output.astype(jnp.bfloat16), "tp").astype(jnp.float32)
    mixed_heads = lax.dynamic_slice_in_dim(whole, lax.axis_index("tp") * width_loc, width_loc, 2)
    resid = local_mods[2][:, None, :] * mixed_heads
    flag = (refresh == 1)[:, None, None]
    new_cache = jnp.where(flag, resid, cache)
    out_img = img.astype(jnp.float32) + new_cache
    return (out_img, new_cache, rel_l1)


def solution(mesh):
    return jax.shard_map(
        local,
        mesh=mesh,
        in_specs=(
            P(None, "seq", "tp"),
            P(None, "seq", "tp"),
            P(None, "seq", "tp"),
            P(None, "seq", "tp"),
            P(None, None, "tp"),
            P("seq", None, "tp"),
            P(None, "tp"),
            P("tp", None),
            P(),
            P(),
        ),
        out_specs=(P(None, "seq", "tp"), P(None, "seq", "tp"), P()),
        check_vma=False,
    )
```

profile of v0, /device:TPU:0, one launch (start us, length us, event | category | flops | bytes accessed | tf_op | source)
XLA Modules:
  0.0 434.7 jit_solution(10169232465015273428)
XLA Ops:
  7.2 0.7 all-gather.3.cloned.1.call-update
  8.0 2.2 all_gather.13
  10.2 1.1 pad_maximum_fusion.1
  11.3 2.5 all_gather.12
  14.1 0.4 fusion.14
  14.5 0.5 fusion.17
  15.0 209.3 %all-gather.3.cloned.1.call-done = bf16[3072,3,1024]{2,0,1:T(8,128)(2,1)} async-done(((bf16[192,3,1024]{2,0,1:T(8,128)(2,1)}), bf16[3072,3,1024]{2,0,1:T(8,128)(2,1)}) %all-gather.3.cloned.1.call-update) | async-done | bytes 18874384 | tf_op jit(solution)/shard_map/all_gather | solution.py:46
  224.3 8.1 %fusion = f32[4,36,3,1024]{3,1,2,0:T(8,128)S(1)} fusion(bf16[3072,3,1024]{2,0,1:T(8,128)(2,1)} %all-gather.3.cloned.1.call-done, bf16[4,36,3072]{2,1,0:T(8,128)(2,1)S(1)} %fusion.17), kind=kOutput, calls=%fused_computation | convolution fusion | flops 2717908992 | bytes 21528576 | tf_op jit(solution)/shard_map/btd,dkc->btkc/dot_general | solution.py:43
  232.4 0.9 slice_multiply_fusion
  233.3 0.8 slice.62
  234.1 1.2 reshape.130
  235.3 0.9 reduce_sum.66
  236.1 1.0 copy.47
  237.2 1.0 mul.103
  238.3 1.3 mul.104
  239.9 1.1 pad_maximum_fusion
  241.0 1.3 copy.50
  242.4 1.1 slice.53
  243.5 1.3 fusion.49
  244.8 40.5 %all-reduce = (f32[4]{0:T(128)S(1)}, f32[4]{0:T(128)S(1)}) all-reduce(f32[4]{0:T(128)S(1)} %get-tuple-element.4, f32[4]{0:T(128)S(1)} %get-tuple-element.3), channel_id=1, replica_groups=mesh['seq'=16,'tp'=2] {'seq','tp'}, use_global_device_ids=true, to_apply=%region_8.9 | all-reduce | flops 8 | bytes 64 | tf_op jit(solution)/shard_map/psum | solution.py:40
  286.0 77.3 %all-gather.5.cloned.1.call-done = bf16[4,576,2,1024]{3,0,2,1:T(4,128)(2,1)} async-done(((bf16[4,36,2,1024]{3,0,2,1:T(4,128)(2,1)}), bf16[4,576,2,1024]{3,0,2,1:T(4,128)(2,1)}) %all-gather.5.cloned.1.call-update) | async-done | bytes 9437200 | tf_op jit(solution)/shard_map/all_gather | solution.py:57
  363.3 10.7 %fusion.70 = (bf16[4,576,1,1024]{3,0,2,1:T(4,128)(2,1)}, bf16[4,576,1,1024]{3,0,2,1:T(4,128)(2,1)}) fusion(bf16[4,576,2,1024]{3,0,2,1:T(4,128)(2,1)} %all-gather.5.cloned.1.call-done), kind=kLoop, calls=%fused_computation.82 | loop fusion | bytes 18874368 | tf_op jit(solution)/shard_map/slice | solution.py:64
  374.0 8.0 %reshape.131 = bf16[4,576,8,128]{3,2,0,1:T(8,128)(2,1)} reshape(bf16[4,576,1,1024]{3,0,2,1:T(4,128)(2,1)} %get-tuple-element.9) | data formatting | bytes 9437184 | tf_op jit(solution)/shard_map/reshape;squeeze | solution.py:64
  382.0 7.5 %fusion.13 = (f32[4,8,32]{2,1,0:T(8,128)S(1)}, f32[4,8,32,576]{3,2,1,0:T(8,128)S(1)}) fusion(pred[4,576]{1,0:T(4,128)(4,1)S(1)} %compare_or_fusion, bf16[4,576,8,128]{3,2,0,1:T(8,128)(2,1)} %reshape.131, bf16[4,32,8,128]{3,2,1,0:T(8,128)(2,1)S(1)} %fusion.54), kind=kOutput, calls=%fused_computation.15 | convolution fusion | flops 152763392 | bytes 7346432 | tf_op jit(solution)/shard_map/bqhc,bkhc->bhqk/dot_general | solution.py:67
  389.5 8.0 %reshape.132 = bf16[4,576,8,128]{3,2,0,1:T(8,128)(2,1)} reshape(bf16[4,576,1,1024]{3,0,2,1:T(4,128)(2,1)} %get-tuple-element.10) | data formatting | bytes 9437184 | tf_op jit(solution)/shard_map/reshape;squeeze | solution.py:65
  397.6 0.8 fusion.18
  398.4 8.1 %fusion.41 = bf16[4,8,4,8,128]{4,3,2,1,0:T(8,128)(2,1)S(1)} fusion(bf16[4,576,8,128]{3,2,0,1:T(8,128)(2,1)} %reshape.132, f32[4,8,32,576]{3,2,1,0:T(8,128)S(1)} %get-tuple-element.16, f32[4,8,32]{2,1,0:T(8,128)S(1)} %broadcast_maximum_fusion, pred[4,576]{1,0:T(4,128)(4,1)S(1)} %compare_or_fusion, f32[4,32,8]{1,2,0:T(8,128)S(1)} %bitcast.67), kind=kOutput, calls=%fused_computation.30 | convolution fusion | flops 154206208 | bytes 7350528 | tf_op jit(solution)/shard_map/bhqk,bkhc->bhqc/dot_general | solution.py:76
  406.6 1.9 fusion.8
  408.5 0.5 maximum_divide_fusion
  409.0 0.7 bitcast_convert_fusion
  409.7 16.1 %all-reduce.3.cloned.1.call-done = bf16[4,32,3072]{2,1,0:T(8,128)(2,1)} async-done(((bf16[4,32,3072]{2,1,0:T(8,128)(2,1)}), bf16[4,32,3072]{2,1,0:T(8,128)(2,1)}) %all-reduce.3.cloned.1.call-update) | async-done | bytes 786448 | tf_op jit(solution)/shard_map/psum | solution.py:88
  425.8 2.4 convert_add_fusion
  (41 shorter events, 1.7 us)
Async XLA Ops:
  7.2 217.1 %all-gather.3.cloned.1.call-start = ((), (), s32[]{:S(2)}) async-start(), calls=%async_computation | async-start | bytes 20054016 | tf_op jit(solution)/shard_map/all_gather | solution.py:46
  7.9 6.6 %copy-start.3 = (f32[2,1024]{1,0:T(2,128)S(1)}, f32[2,1024]{1,0:T(2,128)}, u32[]{:S(2)}) copy-start(f32[2,1024]{1,0:T(2,128)} %param.16) | copy-start | bytes 24580
  7.9 355.4 %all-gather.5.cloned.1.call-start = ((), (), s32[]{:S(2)}) async-start(), calls=%async_computation.1 | async-start | bytes 10027008 | tf_op jit(solution)/shard_map/all_gather | solution.py:57
  239.9 3.6 copy-start.2
  239.9 45.4 %copy-start.4 = (s32[4]{0:T(128)S(1)}, s32[4]{0:T(128)}, u32[]{:S(2)}) copy-start(s32[4]{0:T(128)} %param.18) | copy-start | bytes 52
  242.3 183.5 %all-reduce.3.cloned.1.call-start = ((), (), s32[]{:S(2)}) async-start(), calls=%async_computation.2 | async-start | bytes 1572864 | tf_op jit(solution)/shard_map/psum | solution.py:88
  397.6 8.9 %slice-start = ((s8[6291456]{0:T(1024)(128)(4,1)}), s8[4194304]{0:T(1024)(128)(4,1)S(1)}, s32[]{:S(2)}) async-start(s8[6291456]{0:T(1024)(128)(4,1)} %bitcast.62), calls=%async_computation.3 | async-start | bytes 8388608
  398.4 8.1 %slice-start.1 = ((s8[6291456]{0:T(1024)(128)(4,1)}), s8[2097152]{0:T(1024)(128)(4,1)S(1)}, s32[]{:S(2)}) async-start(s8[6291456]{0:T(1024)(128)(4,1)} %bitcast.62), calls=%async_computation.4 | async-start | bytes 4194304
  406.5 1.9 copy-start.5
  406.5 19.2 %copy-start = (bf16[4,32,1536]{2,1,0:T(8,128)(2,1)S(1)}, bf16[4,32,1536]{2,1,0:T(8,128)(2,1)}, u32[]{:S(2)}) copy-start(bf16[4,32,1536]{2,1,0:T(8,128)(2,1)} %param.10) | copy-start | bytes 1179652
  406.6 19.2 %copy-start.1 = (f32[4,32,1536]{2,1,0:T(8,128)S(1)}, f32[4,32,1536]{2,1,0:T(8,128)}, u32[]{:S(2)}) copy-start(f32[4,32,1536]{2,1,0:T(8,128)} %param.13) | copy-start | bytes 2359300
Sparse Core Ops, SparseCore 0:
  10.6 213.6 all-gather.2
  242.4 120.8 all-gather.4
  408.6 17.1 all-reduce.2
where the time goes:
time: 436 us; the launch traced here: 435 us
  waiting for transfers between devices  303 us (69%)
  blocking collectives  45.3 us (10%)
  local copies, waits for them, and re-layouts  34.7 us (8%)
  matrix products  25.6 us (6%)
  between operations  14 us (3%)
  other arithmetic  11.8 us (3%)
    all_gather x1, waiting for transfers between devices, local(): lax.all_gather(w_qkv, 'seq', axis=0, tiled=True)  209 us
    all_gather x1, waiting for transfers between devices, local(): piece = lax.all_gather(paired, 'seq', axis=1, tiled=True)  77.3 us
    psum x1, blocking collectives, local(): numer, denom = lax.psum((gap, base_sum), ('seq', 'tp'))  40.5 us
    psum x1, waiting for transfers between devices, local(): lax.psum(partial_output.astype(jnp.bfloat16), 'tp').astype(jnp.float32)  16.1 us
    slice x1, local copies, waits for them, and re-layouts, local(): keys = piece[:, :, 0, :].reshape(batch, count, heads, HD)  10.7 us
  transfers between devices with their start and end apart: 3, of which 3 were waited for; matrix products, arithmetic and copies ran while one was open for 2% of the time, Pallas kernels for 0%

commit v1 on v0

--- a/solution.py
+++ b/solution.py
@@ -40,12 +40,38 @@
     numer, denom = lax.psum((gap, base_sum), ("seq", "tp"))
     rel_l1 = numer / jnp.maximum(denom, 1.0)
     columns = w_qkv.shape[2]
-    projected = jnp.einsum(
+    count_2, position, rows_2 = (lax.axis_size("seq"), lax.axis_index("seq"), w_qkv.shape[0])
+    right = [(i, (i + 1) % count_2) for i in range(count_2)]
+    behind = [(i, (i - 1) % count_2) for i in range(count_2)]
+    halfway = count_2 // 2
+    from_left = from_right = w_qkv
+    total_2 = jnp.einsum(
         "btd,dkc->btkc",
-        modded,
-        lax.all_gather(w_qkv, "seq", axis=0, tiled=True),
+        lax.dynamic_slice_in_dim(modded, position * rows_2, w_qkv.shape[0], axis=2),
+        w_qkv,
         preferred_element_type=jnp.float32,
     )
+    for lap in range(1, halfway + 1):
+        from_left = lax.ppermute(from_left, "seq", right)
+        if lap < count_2 - halfway:
+            from_right = lax.ppermute(from_right, "seq", behind)
+            total_2 = total_2 + jnp.einsum(
+                "btd,dkc->btkc",
+                lax.dynamic_slice_in_dim(
+                    modded, (position + lap) % count_2 * rows_2, from_right.shape[0], axis=2
+                ),
+                from_right,
+                preferred_element_type=jnp.float32,
+            )
+        total_2 = total_2 + jnp.einsum(
+            "btd,dkc->btkc",
+            lax.dynamic_slice_in_dim(
+                modded, (position - lap) % count_2 * rows_2, from_left.shape[0], axis=2
+            ),
+            from_left,
+            preferred_element_type=jnp.float32,
+        )
+    projected = total_2
     heads = columns // HD
     query = unit_heads(projected[:, txt_rows:, 0, :], qk_gain[0]).astype(jnp.bfloat16)
     query_heads = query.reshape(batch, img_rows, heads, HD)

time: 436 us -> 607 us (1.39)
  starting transfers between devices: 0.12 us -> 107 us
  waiting for transfers between devices: 303 us -> 349 us
  matrix products: 25.6 us -> 42.6 us
    ppermute x0 -> x15, waiting for transfers between devices: none -> 253 us  [the longest x8 253 us: local(): from_left = lax.ppermute(from_left, 'seq', right)]
    all_gather x1 -> x0, waiting for transfers between devices: 209 us -> none  [local(): lax.all_gather(w_qkv, 'seq', axis=0, tiled=True)]
    ppermute x0 -> x15, starting transfers between devices: none -> 107 us  [the longest x7 86.2 us: local(): from_right = lax.ppermute(from_right, 'seq', behind)]
    dot_general x1 -> x16, matrix products: 8.14 us -> 25.2 us  [the longest x8 16.1 us: local(): jnp.einsum('btd,dkc->btkc', lax.dynamic_slice_in_dim(modded, (position -...]
  transfers between devices with their start and end apart: 3 -> 17, of which waited for: 3 -> 10; matrix products, arithmetic and copies ran while one was open for 2% -> 4% of each run, Pallas kernels for 0% -> 0%
where the time goes in v1:
time: 607 us; the launch traced here: 606 us
  waiting for transfers between devices  349 us (57%)
  starting transfers between devices  107 us (18%)
  blocking collectives  45.8 us (8%)
  matrix products  42.6 us (7%)
  local copies, waits for them, and re-layouts  35.5 us (6%)
  between operations  14.7 us (2%)
  other arithmetic  11.7 us (2%)
    ppermute x8, waiting for transfers between devices, local(): from_left = lax.ppermute(from_left, 'seq', right)  253 us
    ppermute x7, starting transfers between devices, local(): from_right = lax.ppermute(from_right, 'seq', behind)  86.2 us
    all_gather x1, waiting for transfers between devices, local(): piece = lax.all_gather(paired, 'seq', axis=1, tiled=True)  79.3 us
    psum x1, blocking collectives, local(): numer, denom = lax.psum((gap, base_sum), ('seq', 'tp'))  41.5 us
    ppermute x8, starting transfers between devices, local(): from_left = lax.ppermute(from_left, 'seq', right)  20.3 us
    dot_general x8, matrix products, local(): jnp.einsum('btd,dkc->btkc', lax.dynamic_slice_in_dim(modded, (position -...  16.1 us
    psum x1, waiting for transfers between devices, local(): lax.psum(partial_output.astype(jnp.bfloat16), 'tp').astype(jnp.float32)  16.1 us
  transfers between devices with their start and end apart: 17, of which 10 were waited for; matrix products, arithmetic and copies ran while one was open for 4% of the time, Pallas kernels for 0%

profile of v1, /device:TPU:0, one launch (start us, length us, event | category | flops | bytes accessed | tf_op | source)
XLA Modules:
  0.0 605.8 jit_solution(7992602862170081141)
XLA Ops:
  7.2 3.0 collective-permute-start.1
  10.2 4.1 collective-permute-start
  14.3 46.8 %collective-permute-done.1 = bf16[192,3,1024]{2,0,1:T(8,128)(2,1)S(1)} collective-permute-done((bf16[192,3,1024]{2,0,1:T(8,128)(2,1)}, bf16[192,3,1024]{2,0,1:T(8,128)(2,1)S(1)}, u32[]{:S(2)}, u32[]{:S(2)}) %collective-permute-start.1) | collective-permute-done | bytes 1179680 | tf_op jit(solution)/shard_map/ppermute | solution.py:55
  63.4 3.2 collective-permute-start.2
  66.7 46.4 %collective-permute-done.3 = bf16[192,3,1024]{2,0,1:T(8,128)(2,1)S(1)} collective-permute-done((bf16[192,3,1024]{2,0,1:T(8,128)(2,1)S(1)}, bf16[192,3,1024]{2,0,1:T(8,128)(2,1)S(1)}, u32[]{:S(2)}, u32[]{:S(2)}) %collective-permute-start.3) | collective-permute-done | bytes 1179680 | tf_op jit(solution)/shard_map/ppermute | solution.py:55
  113.1 2.5 collective-permute-start.5
  116.7 2.5 all_gather.9
  119.5 3.2 collective-permute-start.4
  122.6 41.7 %collective-permute-done.5 = bf16[192,3,1024]{2,0,1:T(8,128)(2,1)S(1)} collective-permute-done((bf16[192,3,1024]{2,0,1:T(8,128)(2,1)S(1)}, bf16[192,3,1024]{2,0,1:T(8,128)(2,1)S(1)}, u32[]{:S(2)}, u32[]{:S(2)}) %collective-permute-start.5) | collective-permute-done | bytes 1179680 | tf_op jit(solution)/shard_map/ppermute | solution.py:55
  164.4 2.5 collective-permute-start.7
  169.2 3.2 collective-permute-start.6
  172.4 43.1 %collective-permute-done.7 = bf16[192,3,1024]{2,0,1:T(8,128)(2,1)} collective-permute-done((bf16[192,3,1024]{2,0,1:T(8,128)(2,1)S(1)}, bf16[192,3,1024]{2,0,1:T(8,128)(2,1)}, u32[]{:S(2)}, u32[]{:S(2)}) %collective-permute-start.7) | collective-permute-done | bytes 1179680 | tf_op jit(solution)/shard_map/ppermute | solution.py:55
  215.5 2.6 collective-permute-start.9
  220.7 24.6 %collective-permute-start.8 = (bf16[192,3,1024]{2,0,1:T(8,128)(2,1)}, bf16[192,3,1024]{2,0,1:T(8,128)(2,1)S(1)}, u32[]{:S(2)}, u32[]{:S(2)}) collective-permute-start(bf16[192,3,1024]{2,0,1:T(8,128)(2,1)} %collective-permute-done.6), channel_id=1, source_target_pairs={{0,30},{2,0},{4,2},{6,4},{8,6},{10,8},{12,10},{14,12},{16,14},{18,... | collective-permute-start | bytes 3538952 | tf_op jit(solution)/shard_map/ppermute | solution.py:57
  245.8 21.0 %collective-permute-done.9 = bf16[192,3,1024]{2,0,1:T(8,128)(2,1)} collective-permute-done((bf16[192,3,1024]{2,0,1:T(8,128)(2,1)}, bf16[192,3,1024]{2,0,1:T(8,128)(2,1)}, u32[]{:S(2)}, u32[]{:S(2)}) %collective-permute-start.9) | collective-permute-done | bytes 1179680 | tf_op jit(solution)/shard_map/ppermute | solution.py:55
  266.7 2.5 collective-permute-start.11
  272.0 24.6 %collective-permute-start.10 = (bf16[192,3,1024]{2,0,1:T(8,128)(2,1)S(1)}, bf16[192,3,1024]{2,0,1:T(8,128)(2,1)S(1)}, u32[]{:S(2)}, u32[]{:S(2)}) collective-permute-start(bf16[192,3,1024]{2,0,1:T(8,128)(2,1)S(1)} %collective-permute-done.8), channel_id=1, source_target_pairs={{0,30},{2,0},{4,2},{6,4},{8,6},{10,8},{12,10},{14,12},{16,14},{18,... | collective-permute-start | bytes 3538952 | tf_op jit(solution)/shard_map/ppermute | solution.py:57
  297.1 20.1 %collective-permute-done.11 = bf16[192,3,1024]{2,0,1:T(8,128)(2,1)S(1)} collective-permute-done((bf16[192,3,1024]{2,0,1:T(8,128)(2,1)}, bf16[192,3,1024]{2,0,1:T(8,128)(2,1)S(1)}, u32[]{:S(2)}, u32[]{:S(2)}) %collective-permute-start.11) | collective-permute-done | bytes 1179680 | tf_op jit(solution)/shard_map/ppermute | solution.py:55
  323.5 23.4 %collective-permute-start.12 = (bf16[192,3,1024]{2,0,1:T(8,128)(2,1)S(1)}, bf16[192,3,1024]{2,0,1:T(8,128)(2,1)S(1)}, u32[]{:S(2)}, u32[]{:S(2)}) collective-permute-start(bf16[192,3,1024]{2,0,1:T(8,128)(2,1)S(1)} %collective-permute-done.10), channel_id=1, source_target_pairs={{0,30},{2,0},{4,2},{6,4},{8,6},{10,8},{12,10},{14,12},{16,14},{18,... | collective-permute-start | bytes 3538952 | tf_op jit(solution)/shard_map/ppermute | solution.py:57
  347.0 3.0 fusion.38
  350.0 18.5 %collective-permute-done.13 = bf16[192,3,1024]{2,0,1:T(8,128)(2,1)S(1)} collective-permute-done((bf16[192,3,1024]{2,0,1:T(8,128)(2,1)S(1)}, bf16[192,3,1024]{2,0,1:T(8,128)(2,1)S(1)}, u32[]{:S(2)}, u32[]{:S(2)}) %collective-permute-start.13) | collective-permute-done | bytes 1179680 | tf_op jit(solution)/shard_map/ppermute | solution.py:55
  368.5 2.5 collective-permute-start.14
  378.1 15.8 %collective-permute-done.14 = bf16[192,3,1024]{2,0,1:T(8,128)(2,1)} collective-permute-done((bf16[192,3,1024]{2,0,1:T(8,128)(2,1)S(1)}, bf16[192,3,1024]{2,0,1:T(8,128)(2,1)}, u32[]{:S(2)}, u32[]{:S(2)}) %collective-permute-start.14) | collective-permute-done | bytes 1179680 | tf_op jit(solution)/shard_map/ppermute | solution.py:55
  393.8 6.4 %add_add_fusion = f32[4,36,3,1024]{3,1,2,0:T(8,128)S(1)} fusion(f32[4,36,3,1024]{3,1,2,0:T(8,128)} %fusion.30, f32[4,36,3,1024]{3,1,2,0:T(8,128)} %fusion.32, f32[4,36,3,1024]{3,1,2,0:T(8,128)} %fusion.34, f32[4,36,3,1024]{3,1,2,0:T(8,128)} %fusion.36, f32[4,36,3,1024]{3,1,2,0:T(8,128)} %fusion.38, f32[4,36,3,1024]{3,1,2,0:T(8,128)S(1)} %fusion.40, ...), kind=kOutput, calls=%fused_computation.18 | convolution fusion | flops 176504832 | bytes 31539204 | tf_op jit(solution)/shard_map/btd,dkc->btkc/dot_general | solution.py:66
  412.5 41.5 %all-reduce = (f32[4]{0:T(128)S(1)}, f32[4]{0:T(128)S(1)}) all-reduce(f32[4]{0:T(128)S(1)} %get-tuple-element.4, f32[4]{0:T(128)S(1)} %get-tuple-element.3), channel_id=1, replica_groups=mesh['seq'=16,'tp'=2] {'seq','tp'}, use_global_device_ids=true, to_apply=%region_8.9 | all-reduce | flops 8 | bytes 64 | tf_op jit(solution)/shard_map/psum | solution.py:40
  454.7 79.3 %all-gather.2.cloned.1.call-done = bf16[4,576,2,1024]{3,0,2,1:T(4,128)(2,1)} async-done(((bf16[4,36,2,1024]{3,0,2,1:T(4,128)(2,1)}), bf16[4,576,2,1024]{3,0,2,1:T(4,128)(2,1)}) %all-gather.2.cloned.1.call-update) | async-done | bytes 9437200 | tf_op jit(solution)/shard_map/all_gather | solution.py:83
  534.0 10.7 %fusion.146 = (bf16[4,576,1,1024]{3,0,2,1:T(4,128)(2,1)}, bf16[4,576,1,1024]{3,0,2,1:T(4,128)(2,1)}) fusion(bf16[4,576,2,1024]{3,0,2,1:T(4,128)(2,1)} %all-gather.2.cloned.1.call-done), kind=kLoop, calls=%fused_computation.159 | loop fusion | bytes 18874368 | tf_op jit(solution)/shard_map/slice | solution.py:90
  544.8 8.1 %reshape.161 = bf16[4,576,8,128]{3,2,0,1:T(8,128)(2,1)} reshape(bf16[4,576,1,1024]{3,0,2,1:T(4,128)(2,1)} %get-tuple-element.9) | data formatting | bytes 9437184 | tf_op jit(solution)/shard_map/reshape;squeeze | solution.py:90
  552.8 7.5 %fusion.11 = (f32[4,8,32]{2,1,0:T(8,128)S(1)}, f32[4,8,32,576]{3,2,1,0:T(8,128)S(1)}) fusion(pred[4,576]{1,0:T(4,128)(4,1)S(1)} %compare_or_fusion, bf16[4,576,8,128]{3,2,0,1:T(8,128)(2,1)} %reshape.161, bf16[4,32,8,128]{3,2,1,0:T(8,128)(2,1)S(1)} %fusion.82), kind=kOutput, calls=%fused_computation.13 | convolution fusion | flops 152763392 | bytes 7346432 | tf_op jit(solution)/shard_map/bqhc,bkhc->bhqk/dot_general | solution.py:93
  560.3 8.1 %reshape.162 = bf16[4,576,8,128]{3,2,0,1:T(8,128)(2,1)} reshape(bf16[4,576,1,1024]{3,0,2,1:T(4,128)(2,1)} %get-tuple-element.10) | data formatting | bytes 9437184 | tf_op jit(solution)/shard_map/reshape;squeeze | solution.py:91
  569.2 8.1 %fusion.70 = bf16[4,8,4,8,128]{4,3,2,1,0:T(8,128)(2,1)S(1)} fusion(bf16[4,576,8,128]{3,2,0,1:T(8,128)(2,1)} %reshape.162, f32[4,8,32,576]{3,2,1,0:T(8,128)S(1)} %get-tuple-element.16, f32[4,8,32]{2,1,0:T(8,128)S(1)} %broadcast_maximum_fusion, pred[4,576]{1,0:T(4,128)(4,1)S(1)} %compare_or_fusion, f32[4,32,8]{1,2,0:T(8,128)S(1)} %bitcast.187), kind=kOutput, calls=%fused_computation.60 | convolution fusion | flops 154206208 | bytes 7350528 | tf_op jit(solution)/shard_map/bhqk,bkhc->bhqc/dot_general | solution.py:102
  580.5 16.1 %all-reduce.3.cloned.1.call-done = bf16[4,32,3072]{2,1,0:T(8,128)(2,1)} async-done(((bf16[4,32,3072]{2,1,0:T(8,128)(2,1)}), bf16[4,32,3072]{2,1,0:T(8,128)(2,1)}) %all-reduce.3.cloned.1.call-update) | async-done | bytes 786448 | tf_op jit(solution)/shard_map/psum | solution.py:114
  (103 shorter events, 44.8 us)
Async XLA Ops:
  7.2 159.7 %copy-start.12 = (bf16[3,4,1536]{2,1,0:T(4,128)(2,1)S(1)}, bf16[3,4,1536]{2,1,0:T(4,128)(2,1)}, u32[]{:S(2)}) copy-start(bf16[3,4,1536]{2,1,0:T(4,128)(2,1)} %param.14) | copy-start | bytes 110596
  7.2 526.9 %all-gather.2.cloned.1.call-start = ((), (), s32[]{:S(2)}) async-start(), calls=%async_computation | async-start | bytes 10027008 | tf_op jit(solution)/shard_map/all_gather | solution.py:83
  7.2 53.8 %collective-permute-start.1 = (bf16[192,3,1024]{2,0,1:T(8,128)(2,1)}, bf16[192,3,1024]{2,0,1:T(8,128)(2,1)S(1)}, u32[]{:S(2)}, u32[]{:S(2)}) collective-permute-start(bf16[192,3,1024]{2,0,1:T(8,128)(2,1)} %param.15), channel_id=1, source_target_pairs={{0,2},{2,4},{4,6},{6,8},{8,10},{10,12},{12,14},{14,16},{16,18},{18... | collective-permute-start | bytes 3538952 | tf_op jit(solution)/shard_map/ppermute | solution.py:55
  10.2 53.2 %collective-permute-start = (bf16[192,3,1024]{2,0,1:T(8,128)(2,1)}, bf16[192,3,1024]{2,0,1:T(8,128)(2,1)S(1)}, u32[]{:S(2)}, u32[]{:S(2)}) collective-permute-start(bf16[192,3,1024]{2,0,1:T(8,128)(2,1)} %param.15), channel_id=1, source_target_pairs={{0,30},{2,0},{4,2},{6,4},{8,6},{10,8},{12,10},{14,12},{16,14},{18,... | collective-permute-start | bytes 3538952 | tf_op jit(solution)/shard_map/ppermute | solution.py:57
  61.1 52.0 %copy-start.4 = (bf16[192,3,1024]{2,0,1:T(8,128)(2,1)}, bf16[192,3,1024]{2,0,1:T(8,128)(2,1)S(1)}, u32[]{:S(2)}) copy-start(bf16[192,3,1024]{2,0,1:T(8,128)(2,1)S(1)} %collective-permute-done.1) | copy-start | bytes 3538948
  61.1 52.0 %collective-permute-start.3 = (bf16[192,3,1024]{2,0,1:T(8,128)(2,1)S(1)}, bf16[192,3,1024]{2,0,1:T(8,128)(2,1)S(1)}, u32[]{:S(2)}, u32[]{:S(2)}) collective-permute-start(bf16[192,3,1024]{2,0,1:T(8,128)(2,1)S(1)} %collective-permute-done.1), channel_id=1, source_target_pairs={{0,2},{2,4},{4,6},{6,8},{8,10},{10,12},{12,14},{14,16},{16,18},{18... | collective-permute-start | bytes 3538952 | tf_op jit(solution)/shard_map/ppermute | solution.py:55
  63.4 105.7 %copy-start.8 = (bf16[192,3,1024]{2,0,1:T(8,128)(2,1)}, bf16[192,3,1024]{2,0,1:T(8,128)(2,1)S(1)}, u32[]{:S(2)}) copy-start(bf16[192,3,1024]{2,0,1:T(8,128)(2,1)S(1)} %collective-permute-done) | copy-start | bytes 3538948
  63.4 56.0 %collective-permute-start.2 = (bf16[192,3,1024]{2,0,1:T(8,128)(2,1)S(1)}, bf16[192,3,1024]{2,0,1:T(8,128)(2,1)S(1)}, u32[]{:S(2)}, u32[]{:S(2)}) collective-permute-start(bf16[192,3,1024]{2,0,1:T(8,128)(2,1)S(1)} %collective-permute-done), channel_id=1, source_target_pairs={{0,30},{2,0},{4,2},{6,4},{8,6},{10,8},{12,10},{14,12},{16,14},{18,... | collective-permute-start | bytes 3538952 | tf_op jit(solution)/shard_map/ppermute | solution.py:57
  113.1 51.3 %collective-permute-start.5 = (bf16[192,3,1024]{2,0,1:T(8,128)(2,1)S(1)}, bf16[192,3,1024]{2,0,1:T(8,128)(2,1)S(1)}, u32[]{:S(2)}, u32[]{:S(2)}) collective-permute-start(bf16[192,3,1024]{2,0,1:T(8,128)(2,1)S(1)} %collective-permute-done.3), channel_id=1, source_target_pairs={{0,2},{2,4},{4,6},{6,8},{8,10},{10,12},{12,14},{14,16},{16,18},{18... | collective-permute-start | bytes 3538952 | tf_op jit(solution)/shard_map/ppermute | solution.py:55
  119.4 98.6 %copy-start.6 = (bf16[192,3,1024]{2,0,1:T(8,128)(2,1)}, bf16[192,3,1024]{2,0,1:T(8,128)(2,1)S(1)}, u32[]{:S(2)}) copy-start(bf16[192,3,1024]{2,0,1:T(8,128)(2,1)S(1)} %collective-permute-done.2) | copy-start | bytes 3538948
  119.5 49.8 %collective-permute-start.4 = (bf16[192,3,1024]{2,0,1:T(8,128)(2,1)S(1)}, bf16[192,3,1024]{2,0,1:T(8,128)(2,1)}, u32[]{:S(2)}, u32[]{:S(2)}) collective-permute-start(bf16[192,3,1024]{2,0,1:T(8,128)(2,1)S(1)} %collective-permute-done.2), channel_id=1, source_target_pairs={{0,30},{2,0},{4,2},{6,4},{8,6},{10,8},{12,10},{14,12},{16,14},{18,... | collective-permute-start | bytes 3538952 | tf_op jit(solution)/shard_map/ppermute | solution.py:57
  164.4 53.7 %copy-start.2 = (bf16[192,3,1024]{2,0,1:T(8,128)(2,1)}, bf16[192,3,1024]{2,0,1:T(8,128)(2,1)S(1)}, u32[]{:S(2)}) copy-start(bf16[192,3,1024]{2,0,1:T(8,128)(2,1)S(1)} %collective-permute-done.5) | copy-start | bytes 3538948
  164.4 51.1 %collective-permute-start.7 = (bf16[192,3,1024]{2,0,1:T(8,128)(2,1)S(1)}, bf16[192,3,1024]{2,0,1:T(8,128)(2,1)}, u32[]{:S(2)}, u32[]{:S(2)}) collective-permute-start(bf16[192,3,1024]{2,0,1:T(8,128)(2,1)S(1)} %collective-permute-done.5), channel_id=1, source_target_pairs={{0,2},{2,4},{4,6},{6,8},{8,10},{10,12},{12,14},{14,16},{16,18},{18... | collective-permute-start | bytes 3538952 | tf_op jit(solution)/shard_map/ppermute | solution.py:55
  168.7 50.2 %copy-start.13 = (f32[2,1024]{1,0:T(2,128)S(1)}, f32[2,1024]{1,0:T(2,128)}, u32[]{:S(2)}) copy-start(f32[2,1024]{1,0:T(2,128)} %param.16) | copy-start | bytes 24580
  168.7 50.2 %copy-start.1 = (bf16[192,3,1024]{2,0,1:T(8,128)(2,1)S(1)}, bf16[192,3,1024]{2,0,1:T(8,128)(2,1)}, u32[]{:S(2)}) copy-start(bf16[192,3,1024]{2,0,1:T(8,128)(2,1)} %param.15) | copy-start | bytes 3538948
  169.2 51.5 %collective-permute-start.6 = (bf16[192,3,1024]{2,0,1:T(8,128)(2,1)}, bf16[192,3,1024]{2,0,1:T(8,128)(2,1)}, u32[]{:S(2)}, u32[]{:S(2)}) collective-permute-start(bf16[192,3,1024]{2,0,1:T(8,128)(2,1)} %collective-permute-done.4), channel_id=1, source_target_pairs={{0,30},{2,0},{4,2},{6,4},{8,6},{10,8},{12,10},{14,12},{16,14},{18,... | collective-permute-start | bytes 3538952 | tf_op jit(solution)/shard_map/ppermute | solution.py:57
  215.5 51.2 %collective-permute-start.9 = (bf16[192,3,1024]{2,0,1:T(8,128)(2,1)}, bf16[192,3,1024]{2,0,1:T(8,128)(2,1)}, u32[]{:S(2)}, u32[]{:S(2)}) collective-permute-start(bf16[192,3,1024]{2,0,1:T(8,128)(2,1)} %collective-permute-done.7), channel_id=1, source_target_pairs={{0,2},{2,4},{4,6},{6,8},{8,10},{10,12},{12,14},{14,16},{16,18},{18... | collective-permute-start | bytes 3538952 | tf_op jit(solution)/shard_map/ppermute | solution.py:55
  220.2 25.1 %copy-start.5 = (bf16[192,3,1024]{2,0,1:T(8,128)(2,1)S(1)}, bf16[192,3,1024]{2,0,1:T(8,128)(2,1)}, u32[]{:S(2)}) copy-start(bf16[192,3,1024]{2,0,1:T(8,128)(2,1)} %copy-done.4) | copy-start | bytes 3538948
  220.7 48.5 %copy-start.7 = (bf16[192,3,1024]{2,0,1:T(8,128)(2,1)S(1)}, bf16[192,3,1024]{2,0,1:T(8,128)(2,1)}, u32[]{:S(2)}) copy-start(bf16[192,3,1024]{2,0,1:T(8,128)(2,1)} %copy-done.6) | copy-start | bytes 3538948
  220.7 51.3 %collective-permute-start.8 = (bf16[192,3,1024]{2,0,1:T(8,128)(2,1)}, bf16[192,3,1024]{2,0,1:T(8,128)(2,1)S(1)}, u32[]{:S(2)}, u32[]{:S(2)}) collective-permute-start(bf16[192,3,1024]{2,0,1:T(8,128)(2,1)} %collective-permute-done.6), channel_id=1, source_target_pairs={{0,30},{2,0},{4,2},{6,4},{8,6},{10,8},{12,10},{14,12},{16,14},{18,... | collective-permute-start | bytes 3538952 | tf_op jit(solution)/shard_map/ppermute | solution.py:57
  266.7 50.4 %collective-permute-start.11 = (bf16[192,3,1024]{2,0,1:T(8,128)(2,1)}, bf16[192,3,1024]{2,0,1:T(8,128)(2,1)S(1)}, u32[]{:S(2)}, u32[]{:S(2)}) collective-permute-start(bf16[192,3,1024]{2,0,1:T(8,128)(2,1)} %collective-permute-done.9), channel_id=1, source_target_pairs={{0,2},{2,4},{4,6},{6,8},{8,10},{10,12},{12,14},{14,16},{16,18},{18... | collective-permute-start | bytes 3538952 | tf_op jit(solution)/shard_map/ppermute | solution.py:55
  270.2 26.4 %copy-start.3 = (bf16[192,3,1024]{2,0,1:T(8,128)(2,1)S(1)}, bf16[192,3,1024]{2,0,1:T(8,128)(2,1)}, u32[]{:S(2)}) copy-start(bf16[192,3,1024]{2,0,1:T(8,128)(2,1)} %copy-done.2) | copy-start | bytes 3538948
  272.0 51.5 %collective-permute-start.10 = (bf16[192,3,1024]{2,0,1:T(8,128)(2,1)S(1)}, bf16[192,3,1024]{2,0,1:T(8,128)(2,1)S(1)}, u32[]{:S(2)}, u32[]{:S(2)}) collective-permute-start(bf16[192,3,1024]{2,0,1:T(8,128)(2,1)S(1)} %collective-permute-done.8), channel_id=1, source_target_pairs={{0,30},{2,0},{4,2},{6,4},{8,6},{10,8},{12,10},{14,12},{16,14},{18,... | collective-permute-start | bytes 3538952 | tf_op jit(solution)/shard_map/ppermute | solution.py:57
  317.2 51.3 %collective-permute-start.13 = (bf16[192,3,1024]{2,0,1:T(8,128)(2,1)S(1)}, bf16[192,3,1024]{2,0,1:T(8,128)(2,1)S(1)}, u32[]{:S(2)}, u32[]{:S(2)}) collective-permute-start(bf16[192,3,1024]{2,0,1:T(8,128)(2,1)S(1)} %collective-permute-done.11), channel_id=1, source_target_pairs={{0,2},{2,4},{4,6},{6,8},{8,10},{10,12},{12,14},{14,16},{16,18},{18... | collective-permute-start | bytes 3538952 | tf_op jit(solution)/shard_map/ppermute | solution.py:55
  323.5 52.7 %collective-permute-start.12 = (bf16[192,3,1024]{2,0,1:T(8,128)(2,1)S(1)}, bf16[192,3,1024]{2,0,1:T(8,128)(2,1)S(1)}, u32[]{:S(2)}, u32[]{:S(2)}) collective-permute-start(bf16[192,3,1024]{2,0,1:T(8,128)(2,1)S(1)} %collective-permute-done.10), channel_id=1, source_target_pairs={{0,30},{2,0},{4,2},{6,4},{8,6},{10,8},{12,10},{14,12},{16,14},{18,... | collective-permute-start | bytes 3538952 | tf_op jit(solution)/shard_map/ppermute | solution.py:57
  368.5 25.3 %collective-permute-start.14 = (bf16[192,3,1024]{2,0,1:T(8,128)(2,1)S(1)}, bf16[192,3,1024]{2,0,1:T(8,128)(2,1)}, u32[]{:S(2)}, u32[]{:S(2)}) collective-permute-start(bf16[192,3,1024]{2,0,1:T(8,128)(2,1)S(1)} %collective-permute-done.13), channel_id=1, source_target_pairs={{0,2},{2,4},{4,6},{6,8},{8,10},{10,12},{12,14},{14,16},{16,18},{18... | collective-permute-start | bytes 3538952 | tf_op jit(solution)/shard_map/ppermute | solution.py:55
  408.8 45.2 %copy-start.14 = (s32[4]{0:T(128)S(1)}, s32[4]{0:T(128)}, u32[]{:S(2)}) copy-start(s32[4]{0:T(128)} %param.18) | copy-start | bytes 52
  410.1 186.5 %all-reduce.3.cloned.1.call-start = ((), (), s32[]{:S(2)}) async-start(), calls=%async_computation.1 | async-start | bytes 1572864 | tf_op jit(solution)/shard_map/psum | solution.py:114
  568.4 8.9 %slice-start = ((s8[6291456]{0:T(1024)(128)(4,1)}), s8[4194304]{0:T(1024)(128)(4,1)S(1)}, s32[]{:S(2)}) async-start(s8[6291456]{0:T(1024)(128)(4,1)} %bitcast.182), calls=%async_computation.2 | async-start | bytes 8388608
  569.2 8.1 %slice-start.1 = ((s8[6291456]{0:T(1024)(128)(4,1)}), s8[2097152]{0:T(1024)(128)(4,1)S(1)}, s32[]{:S(2)}) async-start(s8[6291456]{0:T(1024)(128)(4,1)} %bitcast.182), calls=%async_computation.3 | async-start | bytes 4194304
  577.3 19.2 %copy-start = (bf16[4,32,1536]{2,1,0:T(8,128)(2,1)S(1)}, bf16[4,32,1536]{2,1,0:T(8,128)(2,1)}, u32[]{:S(2)}) copy-start(bf16[4,32,1536]{2,1,0:T(8,128)(2,1)} %param.10) | copy-start | bytes 1179652
  577.4 19.2 %copy-start.10 = (f32[4,32,1536]{2,1,0:T(8,128)S(1)}, f32[4,32,1536]{2,1,0:T(8,128)}, u32[]{:S(2)}) copy-start(f32[4,32,1536]{2,1,0:T(8,128)} %param.13) | copy-start | bytes 2359300
  (3 other events, 5.7 us)
Sparse Core Ops, SparseCore 0:
  410.2 123.8 all-gather.1
  579.4 17.1 all-reduce.2
